TPU v7x, 32 devices: a whole 2x2x4 slice. The times are simulated.
32 devices in a mesh: pts: 8 (over y, x, core), wlk: 4 (over z).
Axes of the slice: x: 2, y: 2, z: 4, core: 2. Of those that a mesh axis runs over, the one named last changes fastest.
Arguments:
- green_half: bfloat16 [8, 400, 2400], P('wlk'), may hold values from -6 to 6
- collocation: bfloat16 [2400, 9600], P('wlk', 'pts'), may hold values from -0.125 to 0.125
- occupied: bfloat16 [9600, 400], P('pts'), may hold values from -0.0029296875 to 0.0029296875
- kernel: bfloat16 [9600, 9600], P('pts'), may hold values from 0 to 16, as said below
Outputs:
- potential: float32 [8, 9600], P('wlk', 'pts')
- coulomb_energy: float32 [8], P('wlk')
- exchange_energy: float32 [8], P('wlk')
Inputs may be any that keep to these rules, and one draw needn't show every extreme that they name: kernel is symmetric and positive definite: kernel[p, q] equals kernel[q, p].
All inputs are finite; a program needn't handle non-finite values.
Results may differ from a plain program's by a relative error of at most 0.008.
Values may be sent and summed in bfloat16 or wider, within the bound.
A program may use at most 192 MiB of HBM per device.

v0:
```python
import jax
import jax.numpy as jnp
from jax import lax
from jax.sharding import PartitionSpec as P


def passed_along(block, axis, distance):
    devices = range(lax.axis_size(axis))
    route = [((i - distance) % len(devices), i) for i in devices]
    return lax.ppermute(block, axis, route)


def local(green_half, collocation, occupied, kernel):
    pts_rows = occupied.shape[0]
    theta = jnp.einsum(
        "mp,wim->pwi",
        lax.all_gather(collocation, "wlk", axis=0, tiled=True),
        green_half,
        preferred_element_type=jnp.float32,
    ).astype(jnp.bfloat16)
    density = jnp.einsum("pwi,pi->wp", theta, occupied, preferred_element_type=jnp.float32)
    density_b = density.astype(jnp.bfloat16)

    def block_terms(start, theta_far, occ_far):
        cross_near = jnp.einsum("awi,bi->wab", theta, occ_far, preferred_element_type=jnp.float32)
        cross_far = jnp.einsum(
            "ai,bwi->wab", occupied, theta_far, preferred_element_type=jnp.float32
        )
        kernel_part = lax.dynamic_slice_in_dim(kernel, start, occ_far.shape[0], 1).astype(
            jnp.float32
        )
        return jnp.sum(kernel_part[None] * cross_near * cross_far, axis=(1, 2))

    density_all = lax.all_gather(density_b, "pts", axis=1, tiled=True)
    potential = jnp.einsum("wq,aq->wa", density_all, kernel, preferred_element_type=jnp.float32)
    devices = lax.axis_size("pts")
    position = lax.axis_index("pts")
    exchange_sum = block_terms(position * pts_rows, theta, occupied)
    travel = (theta, occupied)
    for stride in range(1, devices // 2 + 1):
        travel = passed_along((travel[0], travel[1]), "pts", 1)
        source = (position - stride) % devices
        weight = 1.0 if 2 * stride == devices else 2.0
        exchange_sum = exchange_sum + weight * block_terms(source * pts_rows, travel[0], travel[1])
    coulomb = 0.5 * jnp.sum(density * potential, axis=1)
    coulomb_energy, exchange_energy = lax.psum((coulomb, -0.5 * exchange_sum), "pts")
    return (potential, coulomb_energy, exchange_energy)


def solution(mesh):
    placed = (P("wlk", None, None), P("wlk", "pts"), P("pts", None), P("pts", None))
    return jax.shard_map(
        local,
        mesh=mesh,
        in_specs=placed,
        out_specs=(P("wlk", "pts"), P("wlk"), P("wlk")),
        check_vma=False,
    )
```

profile of v0, /device:TPU:0, one launch (start us, length us, event | category | flops | bytes accessed | tf_op | source)
XLA Modules:
  0.0 310.9 jit_solution(14020435606796289344)
XLA Ops:
  7.2 0.0 all-gather.3.cloned.1.call-start
  7.2 0.7 all-gather.3.cloned.1.call-update
  7.9 0.5 collective-permute-start
  8.4 15.3 %collective-permute-done = bf16[1200,400]{0,1:T(8,128)(2,1)S(1)} collective-permute-done((bf16[1200,400]{0,1:T(8,128)(2,1)}, bf16[1200,400]{0,1:T(8,128)(2,1)S(1)}, u32[]{:S(2)}, u32[]{:S(2)}) %collective-permute-start) | collective-permute-done | bytes 960032 | tf_op jit(solution)/shard_map/ppermute | solution.py:10
  23.8 3.1 convert.2
  26.8 11.8 %collective-permute-done.2 = bf16[1200,400]{0,1:T(8,128)(2,1)S(1)} collective-permute-done((bf16[1200,400]{0,1:T(8,128)(2,1)S(1)}, bf16[1200,400]{0,1:T(8,128)(2,1)S(1)}, u32[]{:S(2)}, u32[]{:S(2)}) %collective-permute-start.2) | collective-permute-done | bytes 960032 | tf_op jit(solution)/shard_map/ppermute | solution.py:10
  38.6 86.6 %all-gather.3.cloned.1.call-done = bf16[2400,1200]{1,0:T(8,128)(2,1)} async-done(((bf16[600,1200]{1,0:T(8,128)(2,1)}), bf16[2400,1200]{1,0:T(8,128)(2,1)}) %all-gather.3.cloned.1.call-update) | async-done | bytes 5760016 | tf_op jit(solution)/shard_map/all_gather | solution.py:17
  125.2 9.4 %multiply_reduce_fusion = (f32[1200,2]{0,1:T(2,128)S(1)}, bf16[1200,2,400]{0,2,1:T(8,128)(2,1)S(1)}) fusion(f32[1200,400]{0,1:T(8,128)} %convert.2, bf16[2,400,2400]{2,1,0:T(8,128)(2,1)} %param.4, bf16[2400,1200]{1,0:T(8,128)(2,1)} %all-gather.3.cloned.1.call-done), kind=kOutput, calls=%fused_computation.20 | convolution fusion | flops 4611837440 | bytes 13449600 | tf_op jit(solution)/shard_map/mp,wim->pwi/dot_general | solution.py:15
  134.6 0.1 collective-permute-start.1
  134.7 17.5 %dynamic-slice_convert_fusion.3 = (f32[1200,1200]{1,0:T(8,128)}, f32[1200,1200]{1,0:T(8,128)}, f32[1200,1200]{1,0:T(8,128)}, f32[1200,1200]{1,0:T(8,128)}, f32[1200,1200]{1,0:T(8,128)}) fusion(bf16[1200,9600]{1,0:T(8,128)(2,1)} %param.7, s32[]{:T(128)S(6)} %select_n.36, s32[]{:T(128)S(6)} %select_n.38, s32[]{:T(128)S(6)} %select_n.34, s32[]{:T(128)S(6)} %select_n.42, ...), kind=kLoop, calls=%fused_computation.25 | loop fusion | flops 7200000 | bytes 43200020 | tf_op jit(solution)/shard_map/convert_element_type | solution.py:29
  152.1 7.8 %copy.21 = f32[1200,1200]{0,1:T(8,128)} copy(f32[1200,1200]{1,0:T(8,128)} %get-tuple-element.7) | data formatting | bytes 11520000 | tf_op jit(solution)/shard_map/convert_element_type | solution.py:29
  160.0 1.5 collective-permute-start.6
  161.5 16.0 %all-gather = bf16[8,1200,2]{1,2,0:T(2,128)(2,1)S(1)} all-gather(bf16[1,1200,2]{1,2,0:T(2,128)(2,1)S(1)} %fusion.29), channel_id=1, replica_groups=mesh['pts'=8,'wlk'=4] {'pts'}, dimensions={0}, use_global_device_ids=true | all-gather | bytes 43200 | tf_op jit(solution)/shard_map/all_gather | solution.py:34
  177.6 0.2 reshape.12
  177.7 0.0 copy-start
  177.7 11.5 %fusion.28 = (f32[2]{0:T(128)S(1)}, f32[2,1200]{1,0:T(2,128)}) fusion(f32[1200,2]{0,1:T(2,128)S(1)} %get-tuple-element.10, bf16[9600,2]{0,1:T(2,128)(2,1)S(1)} %reshape.12, bf16[1200,9600]{1,0:T(8,128)(2,1)} %param.7), kind=kOutput, calls=%fused_computation.43 | convolution fusion | flops 46084800 | bytes 23097608 | tf_op jit(solution)/shard_map/wq,aq->wa/dot_general | solution.py:35
  189.2 0.4 collective-permute-start.3
  189.6 6.3 %fusion.26 = f32[1200,2,1200]{2,0,1:T(8,128)} fusion(bf16[1200,2,400]{0,2,1:T(8,128)(2,1)S(1)} %get-tuple-element.11, bf16[1200,400]{0,1:T(8,128)(2,1)S(1)} %copy-done), kind=kOutput, calls=%fused_computation.39 | convolution fusion | flops 2304000000 | bytes 14400000 | tf_op jit(solution)/shard_map/awi,bi->wab/dot_general | solution.py:25
  195.9 13.4 %copy.22 = f32[1200,2,1200]{0,2,1:T(8,128)} copy(f32[1200,2,1200]{2,0,1:T(8,128)} %fusion.26) | data formatting | bytes 23040000 | tf_op jit(solution)/shard_map/awi,bi->wab/dot_general | solution.py:25
  209.3 10.9 %fusion.8 = f32[2]{0:T(128)S(1)} fusion(f32[1200,2,1200]{2,0,1:T(8,128)} %fusion.26, f32[1200,2,1200]{0,2,1:T(8,128)} %copy.22, f32[1200,1200]{0,1:T(8,128)} %copy.21), kind=kLoop, calls=%fused_computation.17 | loop fusion | flops 8639998 | bytes 28800008 | tf_op jit(solution)/shard_map/reduce_sum | solution.py:32
  220.3 1.5 collective-permute-start.5
  221.8 8.0 %convolution_bitcast_fusion.3 = f32[2,1200,1200]{2,1,0:T(8,128)} fusion(bf16[1200,2,400]{0,2,1:T(8,128)(2,1)} %collective-permute-done.1, bf16[1200,400]{0,1:T(8,128)(2,1)S(1)} %copy-done), kind=kOutput, calls=%fused_computation.15 | convolution fusion | flops 2304000000 | bytes 14400000 | tf_op jit(solution)/shard_map/ai,bwi->wab/dot_general | solution.py:26
  229.8 8.6 %fusion.17 = f32[2]{0:T(128)S(1)} fusion(f32[2,1200,1200]{2,1,0:T(8,128)} %convolution_bitcast_fusion.3, bf16[1200,2,400]{0,2,1:T(8,128)(2,1)S(1)} %get-tuple-element.11, f32[1200,1200]{1,0:T(8,128)S(1)} %bitcast.102, bf16[1200,400]{0,1:T(8,128)(2,1)S(1)} %copy-done.4), kind=kOutput, calls=%fused_computation.30 | convolution fusion | flops 2312640000 | bytes 20160008 | tf_op jit(solution)/shard_map/awi,bi->wab/dot_general | solution.py:25
  238.4 8.2 %convolution_bitcast_fusion.2 = f32[2,1200,1200]{2,1,0:T(8,128)} fusion(bf16[1200,2,400]{0,2,1:T(8,128)(2,1)} %collective-permute-done.3, bf16[1200,400]{0,1:T(8,128)(2,1)S(1)} %copy-done), kind=kOutput, calls=%fused_computation.14 | convolution fusion | flops 2304000000 | bytes 14400000 | tf_op jit(solution)/shard_map/ai,bwi->wab/dot_general | solution.py:26
  246.6 0.3 collective-permute-start.7
  246.9 8.6 %fusion.16 = f32[2]{0:T(128)S(1)} fusion(f32[2,1200,1200]{2,1,0:T(8,128)} %convolution_bitcast_fusion.2, bf16[1200,2,400]{0,2,1:T(8,128)(2,1)S(1)} %get-tuple-element.11, f32[1200,1200]{1,0:T(8,128)S(1)} %bitcast.100, bf16[1200,400]{0,1:T(8,128)(2,1)S(1)} %copy-done.2), kind=kOutput, calls=%fused_computation.29 | convolution fusion | flops 2312640000 | bytes 20160008 | tf_op jit(solution)/shard_map/awi,bi->wab/dot_general | solution.py:25
  255.5 8.1 %convolution_bitcast_fusion.1 = f32[2,1200,1200]{2,1,0:T(8,128)} fusion(bf16[1200,2,400]{0,2,1:T(8,128)(2,1)} %collective-permute-done.5, bf16[1200,400]{0,1:T(8,128)(2,1)S(1)} %copy-done), kind=kOutput, calls=%fused_computation.13 | convolution fusion | flops 2304000000 | bytes 14400000 | tf_op jit(solution)/shard_map/ai,bwi->wab/dot_general | solution.py:26
  263.6 8.9 %fusion.15 = f32[2]{0:T(128)S(1)} fusion(f32[2,1200,1200]{2,1,0:T(8,128)} %convolution_bitcast_fusion.1, bf16[1200,2,400]{0,2,1:T(8,128)(2,1)S(1)} %get-tuple-element.11, f32[1200,1200]{1,0:T(8,128)S(1)} %bitcast.98, bf16[1200,400]{0,1:T(8,128)(2,1)} %collective-permute-done.4), kind=kOutput, calls=%fused_computation.28 | convolution fusion | flops 2312640000 | bytes 20160008 | tf_op jit(solution)/shard_map/awi,bi->wab/dot_general | solution.py:25
  272.5 0.2 collective-permute-done.7
  272.7 8.1 %convolution_bitcast_fusion = f32[2,1200,1200]{2,1,0:T(8,128)} fusion(bf16[1200,2,400]{0,2,1:T(8,128)(2,1)} %collective-permute-done.7, bf16[1200,400]{0,1:T(8,128)(2,1)S(1)} %copy-done), kind=kOutput, calls=%fused_computation.12 | convolution fusion | flops 2304000000 | bytes 14400000 | tf_op jit(solution)/shard_map/ai,bwi->wab/dot_general | solution.py:26
  280.8 8.7 %fusion.14 = f32[2]{0:T(128)S(1)} fusion(f32[2,1200,1200]{2,1,0:T(8,128)} %convolution_bitcast_fusion, bf16[1200,2,400]{0,2,1:T(8,128)(2,1)S(1)} %get-tuple-element.11, f32[1200,1200]{1,0:T(8,128)S(1)} %bitcast.96, bf16[1200,400]{0,1:T(8,128)(2,1)} %collective-permute-done.6), kind=kOutput, calls=%fused_computation.27 | convolution fusion | flops 2312640000 | bytes 20160008 | tf_op jit(solution)/shard_map/awi,bi->wab/dot_general | solution.py:25
  289.6 14.5 %all-reduce = (f32[2]{0:T(128)}, f32[2]{0:T(128)}) all-reduce(f32[2]{0:T(128)S(1)} %broadcast_multiply_fusion, f32[2]{0:T(128)S(1)} %add_multiply_fusion), channel_id=1, replica_groups=mesh['pts'=8,'wlk'=4] {'pts'}, use_global_device_ids=true, to_apply=%region_1.2 | all-reduce | flops 4 | bytes 32 | tf_op jit(solution)/shard_map/psum | solution.py:46
  (40 shorter events, 0.1 us)
Async XLA Ops:
  7.2 118.0 %all-gather.3.cloned.1.call-start = ((), (), s32[]{:S(2)}) async-start(), calls=%async_computation | async-start | bytes 7680000 | tf_op jit(solution)/shard_map/all_gather | solution.py:17
  7.9 15.8 %collective-permute-start = (bf16[1200,400]{0,1:T(8,128)(2,1)}, bf16[1200,400]{0,1:T(8,128)(2,1)S(1)}, u32[]{:S(2)}, u32[]{:S(2)}) collective-permute-start(bf16[1200,400]{0,1:T(8,128)(2,1)} %param.6), channel_id=1, source_target_pairs={{28,0},{0,4},{4,8},{8,12},{12,16},{16,20},{20,24},{24,28},{29,1},{... | collective-permute-start | bytes 2880008 | tf_op jit(solution)/shard_map/ppermute | solution.py:10
  23.7 14.9 %copy-start.3 = (bf16[1200,400]{0,1:T(8,128)(2,1)}, bf16[1200,400]{0,1:T(8,128)(2,1)S(1)}, u32[]{:S(2)}) copy-start(bf16[1200,400]{0,1:T(8,128)(2,1)S(1)} %collective-permute-done) | copy-start | bytes 2880004
  23.7 14.9 %collective-permute-start.2 = (bf16[1200,400]{0,1:T(8,128)(2,1)S(1)}, bf16[1200,400]{0,1:T(8,128)(2,1)S(1)}, u32[]{:S(2)}, u32[]{:S(2)}) collective-permute-start(bf16[1200,400]{0,1:T(8,128)(2,1)S(1)} %collective-permute-done), channel_id=1, source_target_pairs={{28,0},{0,4},{4,8},{8,12},{12,16},{16,20},{20,24},{24,28},{29,1},{... | collective-permute-start | bytes 2880008 | tf_op jit(solution)/shard_map/ppermute | solution.py:10
  38.6 96.0 %copy-start.1 = (bf16[1200,400]{0,1:T(8,128)(2,1)}, bf16[1200,400]{0,1:T(8,128)(2,1)S(1)}, u32[]{:S(2)}) copy-start(bf16[1200,400]{0,1:T(8,128)(2,1)S(1)} %collective-permute-done.2) | copy-start | bytes 2880004
  38.6 121.4 %collective-permute-start.4 = (bf16[1200,400]{0,1:T(8,128)(2,1)S(1)}, bf16[1200,400]{0,1:T(8,128)(2,1)}, u32[]{:S(2)}, u32[]{:S(2)}) collective-permute-start(bf16[1200,400]{0,1:T(8,128)(2,1)S(1)} %collective-permute-done.2), channel_id=1, source_target_pairs={{28,0},{0,4},{4,8},{8,12},{12,16},{16,20},{20,24},{24,28},{29,1},{... | collective-permute-start | bytes 2880008 | tf_op jit(solution)/shard_map/ppermute | solution.py:10
  134.6 54.6 %collective-permute-start.1 = (bf16[1200,2,400]{0,2,1:T(8,128)(2,1)S(1)}, bf16[1200,2,400]{0,2,1:T(8,128)(2,1)}, u32[]{:S(2)}, u32[]{:S(2)}) collective-permute-start(bf16[1200,2,400]{0,2,1:T(8,128)(2,1)S(1)} %get-tuple-element.11), channel_id=1, source_target_pairs={{28,0},{0,4},{4,8},{8,12},{12,16},{16,20},{20,24},{24,28},{29,1},{... | collective-permute-start | bytes 5760008 | tf_op jit(solution)/shard_map/ppermute | solution.py:10
  160.0 120.9 %collective-permute-start.6 = (bf16[1200,400]{0,1:T(8,128)(2,1)}, bf16[1200,400]{0,1:T(8,128)(2,1)}, u32[]{:S(2)}, u32[]{:S(2)}) collective-permute-start(bf16[1200,400]{0,1:T(8,128)(2,1)} %collective-permute-done.4), channel_id=1, source_target_pairs={{28,0},{0,4},{4,8},{8,12},{12,16},{16,20},{20,24},{24,28},{29,1},{... | collective-permute-start | bytes 2880008 | tf_op jit(solution)/shard_map/ppermute | solution.py:10
  177.7 11.9 %copy-start = (bf16[1200,400]{0,1:T(8,128)(2,1)S(1)}, bf16[1200,400]{0,1:T(8,128)(2,1)}, u32[]{:S(2)}) copy-start(bf16[1200,400]{0,1:T(8,128)(2,1)} %param.6) | copy-start | bytes 2880004
  189.2 31.0 %collective-permute-start.3 = (bf16[1200,2,400]{0,2,1:T(8,128)(2,1)}, bf16[1200,2,400]{0,2,1:T(8,128)(2,1)}, u32[]{:S(2)}, u32[]{:S(2)}) collective-permute-start(bf16[1200,2,400]{0,2,1:T(8,128)(2,1)} %collective-permute-done.1), channel_id=1, source_target_pairs={{28,0},{0,4},{4,8},{8,12},{12,16},{16,20},{20,24},{24,28},{29,1},{... | collective-permute-start | bytes 5760008 | tf_op jit(solution)/shard_map/ppermute | solution.py:10
  209.3 20.4 %slice-start.6 = ((s8[6144000]{0:T(1024)(128)(4,1)}), s8[4194304]{0:T(1024)(128)(4,1)S(1)}, s32[]{:S(2)}) async-start(s8[6144000]{0:T(1024)(128)(4,1)} %bitcast.101), calls=%async_computation.7 | async-start | bytes 8388608
  220.3 9.5 %slice-start.7 = ((s8[6144000]{0:T(1024)(128)(4,1)}), s8[1949696]{0:T(1024)(128)(4,1)S(1)}, s32[]{:S(2)}) async-start(s8[6144000]{0:T(1024)(128)(4,1)} %bitcast.101), calls=%async_computation.8 | async-start | bytes 3899392
  220.3 9.5 %copy-start.4 = (bf16[1200,400]{0,1:T(8,128)(2,1)S(1)}, bf16[1200,400]{0,1:T(8,128)(2,1)}, u32[]{:S(2)}) copy-start(bf16[1200,400]{0,1:T(8,128)(2,1)} %copy-done.3) | copy-start | bytes 2880004
  220.3 26.3 %collective-permute-start.5 = (bf16[1200,2,400]{0,2,1:T(8,128)(2,1)}, bf16[1200,2,400]{0,2,1:T(8,128)(2,1)}, u32[]{:S(2)}, u32[]{:S(2)}) collective-permute-start(bf16[1200,2,400]{0,2,1:T(8,128)(2,1)} %collective-permute-done.3), channel_id=1, source_target_pairs={{28,0},{0,4},{4,8},{8,12},{12,16},{16,20},{20,24},{24,28},{29,1},{... | collective-permute-start | bytes 5760008 | tf_op jit(solution)/shard_map/ppermute | solution.py:10
  229.8 17.1 %slice-start.4 = ((s8[6144000]{0:T(1024)(128)(4,1)}), s8[4194304]{0:T(1024)(128)(4,1)S(1)}, s32[]{:S(2)}) async-start(s8[6144000]{0:T(1024)(128)(4,1)} %bitcast.99), calls=%async_computation.5 | async-start | bytes 8388608
  238.4 8.5 %slice-start.5 = ((s8[6144000]{0:T(1024)(128)(4,1)}), s8[1949696]{0:T(1024)(128)(4,1)S(1)}, s32[]{:S(2)}) async-start(s8[6144000]{0:T(1024)(128)(4,1)} %bitcast.99), calls=%async_computation.6 | async-start | bytes 3899392
  238.4 8.5 %copy-start.2 = (bf16[1200,400]{0,1:T(8,128)(2,1)S(1)}, bf16[1200,400]{0,1:T(8,128)(2,1)}, u32[]{:S(2)}) copy-start(bf16[1200,400]{0,1:T(8,128)(2,1)} %copy-done.1) | copy-start | bytes 2880004
  246.6 26.1 %collective-permute-start.7 = (bf16[1200,2,400]{0,2,1:T(8,128)(2,1)}, bf16[1200,2,400]{0,2,1:T(8,128)(2,1)}, u32[]{:S(2)}, u32[]{:S(2)}) collective-permute-start(bf16[1200,2,400]{0,2,1:T(8,128)(2,1)} %collective-permute-done.5), channel_id=1, source_target_pairs={{28,0},{0,4},{4,8},{8,12},{12,16},{16,20},{20,24},{24,28},{29,1},{... | collective-permute-start | bytes 5760008 | tf_op jit(solution)/shard_map/ppermute | solution.py:10
  246.9 16.7 %slice-start.2 = ((s8[6144000]{0:T(1024)(128)(4,1)}), s8[4194304]{0:T(1024)(128)(4,1)S(1)}, s32[]{:S(2)}) async-start(s8[6144000]{0:T(1024)(128)(4,1)} %bitcast.97), calls=%async_computation.3 | async-start | bytes 8388608
  255.5 8.2 %slice-start.3 = ((s8[6144000]{0:T(1024)(128)(4,1)}), s8[1949696]{0:T(1024)(128)(4,1)S(1)}, s32[]{:S(2)}) async-start(s8[6144000]{0:T(1024)(128)(4,1)} %bitcast.97), calls=%async_computation.4 | async-start | bytes 3899392
  263.6 17.2 %slice-start = ((s8[6144000]{0:T(1024)(128)(4,1)}), s8[4194304]{0:T(1024)(128)(4,1)S(1)}, s32[]{:S(2)}) async-start(s8[6144000]{0:T(1024)(128)(4,1)} %bitcast.95), calls=%async_computation.1 | async-start | bytes 8388608
  272.5 8.3 %slice-start.1 = ((s8[6144000]{0:T(1024)(128)(4,1)}), s8[1949696]{0:T(1024)(128)(4,1)S(1)}, s32[]{:S(2)}) async-start(s8[6144000]{0:T(1024)(128)(4,1)} %bitcast.95), calls=%async_computation.2 | async-start | bytes 3899392
Sparse Core Ops, SparseCore 0:
  9.5 115.6 all-gather.2
where the time goes:
time: 312 us; the launch traced here: 311 us
  waiting for transfers between devices  115 us (37%)
  matrix products  94.4 us (30%)
  other arithmetic  31.5 us (10%)
  blocking collectives  30.5 us (10%)
  local copies, waits for them, and re-layouts  21.5 us (7%)
  between operations  14.1 us (5%)
  starting transfers between devices  4.4 us (1%)
    all_gather x1, waiting for transfers between devices, local(): lax.all_gather(collocation, 'wlk', axis=0, tiled=True)  86.6 us
    dot_general x5, matrix products, block_terms(): jnp.einsum('awi,bi->wab', theta, occ_far, preferred_element_type=jnp.floa...  41.1 us
    dot_general x4, matrix products, block_terms(): jnp.einsum('ai,bwi->wab', occupied, theta_far, preferred_element_type=jnp...  32.4 us
    ppermute x8, waiting for transfers between devices, passed_along(): return lax.ppermute(block, axis, route)  27.3 us
    convert_element_type x1, other arithmetic, block_terms(): lax.dynamic_slice_in_dim(kernel, start, occ_far.shape[0], 1)  17.5 us
    all_gather x1, blocking collectives, local(): density_all = lax.all_gather(density_b, 'pts', axis=1, tiled=True)  16 us
    psum x1, blocking collectives, local(): lax.psum((coulomb, -0.5 * exchange_sum), 'pts')  14.5 us
    dot_general x1, local copies, waits for them, and re-layouts, block_terms(): jnp.einsum('awi,bi->wab', theta, occ_far, preferred_element_type=jnp.floa...  13.4 us
  transfers between devices with their start and end apart: 9, of which 4 were waited for; matrix products, arithmetic and copies ran while one was open for 45% of the time, Pallas kernels for 0%

commit v1 on v0

--- a/solution.py
+++ b/solution.py
@@ -2,6 +2,18 @@
 import jax.numpy as jnp
 from jax import lax
 from jax.sharding import PartitionSpec as P
+
+
+def ring_product(x, axis, dim, contribution):
+    size, index = (lax.axis_size(axis), lax.axis_index(axis))
+    downward = [(i, (i - 1) % size) for i in range(size)]
+    rows = x.shape[dim]
+    held = x
+    total = contribution(held, index * rows)
+    for step in range(1, size):
+        held = lax.ppermute(held, axis, downward)
+        total = total + contribution(held, (index + step) % size * rows)
+    return total
 
 
 def passed_along(block, axis, distance):
@@ -12,11 +24,16 @@
 
 def local(green_half, collocation, occupied, kernel):
     pts_rows = occupied.shape[0]
-    theta = jnp.einsum(
-        "mp,wim->pwi",
-        lax.all_gather(collocation, "wlk", axis=0, tiled=True),
-        green_half,
-        preferred_element_type=jnp.float32,
+    theta = ring_product(
+        collocation,
+        "wlk",
+        0,
+        lambda part, start_2: jnp.einsum(
+            "mp,wim->pwi",
+            part,
+            lax.dynamic_slice_in_dim(green_half, start_2, part.shape[0], axis=2),
+            preferred_element_type=jnp.float32,
+        ),
     ).astype(jnp.bfloat16)
     density = jnp.einsum("pwi,pi->wp", theta, occupied, preferred_element_type=jnp.float32)
     density_b = density.astype(jnp.bfloat16)

time: 312 us -> 286 us (0.917)
  waiting for transfers between devices: 115 us -> 84.5 us
  between operations: 14.1 us -> 0.84 us
  starting transfers between devices: 4.4 us -> 16.7 us
  matrix products: 94.4 us -> 97.9 us
    all_gather x1 -> x0, waiting for transfers between devices: 86.6 us -> none  [local(): lax.all_gather(collocation, 'wlk', axis=0, tiled=True)]
    ppermute x0 -> x3, waiting for transfers between devices: none -> 78.1 us  [ring_product(): held = lax.ppermute(held, axis, downward)]
    ppermute x8, waiting for transfers between devices: 27.3 us -> 6.33 us  [passed_along(): return lax.ppermute(block, axis, route)]
    ppermute x0 -> x3, starting transfers between devices: none -> 13.7 us  [ring_product(): held = lax.ppermute(held, axis, downward)]
    dot_general x1 -> x4, matrix products: 9.38 us -> 12.8 us  [local(): jnp.einsum('mp,wim->pwi', part, lax.dynamic_slice_in_dim(green_half, star...]
  transfers between devices with their start and end apart: 9 -> 11, of which waited for: 4 -> 5; matrix products, arithmetic and copies ran while one was open for 45% -> 50% of each run, Pallas kernels for 0% -> 0%
where the time goes in v1:
time: 286 us; the launch traced here: 285 us
  matrix products  97.9 us (34%)
  waiting for transfers between devices  84.5 us (30%)
  other arithmetic  32.1 us (11%)
  blocking collectives  31.2 us (11%)
  local copies, waits for them, and re-layouts  21.5 us (8%)
  starting transfers between devices  16.7 us (6%)
    ppermute x3, waiting for transfers between devices, ring_product(): held = lax.ppermute(held, axis, downward)  78.1 us
    dot_general x5, matrix products, block_terms(): jnp.einsum('awi,bi->wab', theta, occ_far, preferred_element_type=jnp.floa...  41.1 us
    dot_general x4, matrix products, block_terms(): jnp.einsum('ai,bwi->wab', occupied, theta_far, preferred_element_type=jnp...  32.6 us
    convert_element_type x1, other arithmetic, block_terms(): lax.dynamic_slice_in_dim(kernel, start, occ_far.shape[0], 1)  18.1 us
    all_gather x1, blocking collectives, local(): density_all = lax.all_gather(density_b, 'pts', axis=1, tiled=True)  16.7 us
    psum x1, blocking collectives, local(): lax.psum((coulomb, -0.5 * exchange_sum), 'pts')  14.6 us
    ppermute x3, starting transfers between devices, ring_product(): held = lax.ppermute(held, axis, downward)  13.7 us
    dot_general x1, local copies, waits for them, and re-layouts, block_terms(): jnp.einsum('awi,bi->wab', theta, occ_far, preferred_element_type=jnp.floa...  13.4 us
  transfers between devices with their start and end apart: 11, of which 5 were waited for; matrix products, arithmetic and copies ran while one was open for 50% of the time, Pallas kernels for 0%

profile of v1, /device:TPU:0, one launch (start us, length us, event | category | flops | bytes accessed | tf_op | source)
XLA Modules:
  0.0 284.8 jit_solution(14850563744657799469)
XLA Ops:
  0.6 5.1 %collective-permute-start = (bf16[600,1200]{1,0:T(8,128)(2,1)}, bf16[600,1200]{1,0:T(8,128)(2,1)S(1)}, u32[]{:S(2)}, u32[]{:S(2)}) collective-permute-start(bf16[600,1200]{1,0:T(8,128)(2,1)} %param.5), channel_id=1, source_target_pairs={{0,3},{1,0},{2,1},{3,2},{4,7},{5,4},{6,5},{7,6},{8,11},{9,8},{10,9... | collective-permute-start | bytes 4320008 | tf_op jit(solution)/shard_map/ppermute | solution.py:14
  5.8 33.2 %collective-permute-done = bf16[600,1200]{1,0:T(8,128)(2,1)S(1)} collective-permute-done((bf16[600,1200]{1,0:T(8,128)(2,1)}, bf16[600,1200]{1,0:T(8,128)(2,1)S(1)}, u32[]{:S(2)}, u32[]{:S(2)}) %collective-permute-start) | collective-permute-done | bytes 1440032 | tf_op jit(solution)/shard_map/ppermute | solution.py:14
  38.9 4.2 %collective-permute-start.1 = (bf16[600,1200]{1,0:T(8,128)(2,1)S(1)}, bf16[600,1200]{1,0:T(8,128)(2,1)}, u32[]{:S(2)}, u32[]{:S(2)}) collective-permute-start(bf16[600,1200]{1,0:T(8,128)(2,1)S(1)} %collective-permute-done), channel_id=1, source_target_pairs={{0,3},{1,0},{2,1},{3,2},{4,7},{5,4},{6,5},{7,6},{8,11},{9,8},{10,9... | collective-permute-start | bytes 4320008 | tf_op jit(solution)/shard_map/ppermute | solution.py:14
  43.1 32.0 %collective-permute-done.1 = bf16[600,1200]{1,0:T(8,128)(2,1)} collective-permute-done((bf16[600,1200]{1,0:T(8,128)(2,1)S(1)}, bf16[600,1200]{1,0:T(8,128)(2,1)}, u32[]{:S(2)}, u32[]{:S(2)}) %collective-permute-start.1) | collective-permute-done | bytes 1440032 | tf_op jit(solution)/shard_map/ppermute | solution.py:14
  75.1 4.4 %collective-permute-start.2 = (bf16[600,1200]{1,0:T(8,128)(2,1)}, bf16[600,1200]{1,0:T(8,128)(2,1)}, u32[]{:S(2)}, u32[]{:S(2)}) collective-permute-start(bf16[600,1200]{1,0:T(8,128)(2,1)} %collective-permute-done.1), channel_id=1, source_target_pairs={{0,3},{1,0},{2,1},{3,2},{4,7},{5,4},{6,5},{7,6},{8,11},{9,8},{10,9... | collective-permute-start | bytes 4320008 | tf_op jit(solution)/shard_map/ppermute | solution.py:14
  79.6 3.0 %convert.2 = f32[1200,400]{0,1:T(8,128)} convert(bf16[1200,400]{0,1:T(8,128)(2,1)} %param.6) | non-fusion elementwise | flops 480000 | bytes 2880000
  82.6 3.7 %fusion.18 = f32[2,400,1200]{2,1,0:T(8,128)S(1)} fusion(bf16[600,1200]{1,0:T(8,128)(2,1)} %param.5, bf16[2,400,2400]{2,1,0:T(8,128)(2,1)} %param.4, s32[]{:T(128)S(6)} %select_n.58), kind=kOutput, calls=%fused_computation.34 | convolution fusion | flops 1152000000 | bytes 6400004 | tf_op jit(solution)/shard_map/mp,wim->pwi/dot_general | solution.py:31
  86.3 1.8 fusion.16
  88.2 6.2 %collective-permute-done.5 = bf16[1200,400]{0,1:T(8,128)(2,1)S(1)} collective-permute-done((bf16[1200,400]{0,1:T(8,128)(2,1)S(1)}, bf16[1200,400]{0,1:T(8,128)(2,1)S(1)}, u32[]{:S(2)}, u32[]{:S(2)}) %collective-permute-start.5) | collective-permute-done | bytes 960032 | tf_op jit(solution)/shard_map/ppermute | solution.py:22
  94.4 3.6 %fusion.14 = f32[2,400,1200]{2,1,0:T(8,128)S(1)} fusion(bf16[600,1200]{1,0:T(8,128)(2,1)} %collective-permute-done.1, bf16[2,400,2400]{2,1,0:T(8,128)(2,1)S(1)} %copy-done.9, s32[]{:T(128)S(6)} %select_n.62), kind=kOutput, calls=%fused_computation.30 | convolution fusion | flops 1152000000 | bytes 6304004 | tf_op jit(solution)/shard_map/mp,wim->pwi/dot_general | solution.py:31
  98.0 12.9 %collective-permute-done.2 = bf16[600,1200]{1,0:T(8,128)(2,1)} collective-permute-done((bf16[600,1200]{1,0:T(8,128)(2,1)}, bf16[600,1200]{1,0:T(8,128)(2,1)}, u32[]{:S(2)}, u32[]{:S(2)}) %collective-permute-start.2) | collective-permute-done | bytes 1440032 | tf_op jit(solution)/shard_map/ppermute | solution.py:14
  111.0 3.6 %multiply_reduce_fusion = (f32[1200,2]{0,1:T(2,128)S(1)}, bf16[2,400,1200]{2,1,0:T(8,128)(2,1)S(1)}) fusion(f32[1200,400]{0,1:T(8,128)S(1)} %copy-done.3, bf16[600,1200]{1,0:T(8,128)(2,1)} %collective-permute-done.2, bf16[2,400,2400]{2,1,0:T(8,128)(2,1)S(1)} %copy-done.9, s32[]{:T(128)S(6)} %select_n.64, f32[2,400,1200]{2,1,0:T(8,128)S(1)} %fusion.14, ...), kind=kOutput, calls=%fused_computation.18 | convolution fusion | flops 1158717568 | bytes 18729604 | tf_op jit(solution)/shard_map/mp,wim->pwi/dot_general | solution.py:31
  114.7 18.1 %dynamic-slice_convert_fusion.3 = (f32[1200,1200]{1,0:T(8,128)}, f32[1200,1200]{1,0:T(8,128)}, f32[1200,1200]{1,0:T(8,128)}, f32[1200,1200]{1,0:T(8,128)}, f32[1200,1200]{1,0:T(8,128)}) fusion(bf16[1200,9600]{1,0:T(8,128)(2,1)} %param.7, s32[]{:T(128)S(6)} %select_n.67, s32[]{:T(128)S(6)} %select_n.69, s32[]{:T(128)S(6)} %select_n.65, s32[]{:T(128)S(6)} %select_n.73, ...), kind=kLoop, calls=%fused_computation.23 | loop fusion | flops 7200000 | bytes 43200020 | tf_op jit(solution)/shard_map/convert_element_type | solution.py:46
  132.8 7.9 %copy.21 = f32[1200,1200]{0,1:T(8,128)} copy(f32[1200,1200]{1,0:T(8,128)} %get-tuple-element.7) | data formatting | bytes 11520000 | tf_op jit(solution)/shard_map/convert_element_type | solution.py:46
  140.7 0.9 collective-permute-start.9
  141.6 16.7 %all-gather = bf16[8,1200,2]{1,2,0:T(2,128)(2,1)S(1)} all-gather(bf16[1,1200,2]{1,2,0:T(2,128)(2,1)S(1)} %fusion.35), channel_id=1, replica_groups=mesh['pts'=8,'wlk'=4] {'pts'}, dimensions={0}, use_global_device_ids=true | all-gather | bytes 43200 | tf_op jit(solution)/shard_map/all_gather | solution.py:51
  158.5 11.5 %fusion.34 = (f32[2]{0:T(128)S(1)}, f32[2,1200]{1,0:T(2,128)}) fusion(f32[1200,2]{0,1:T(2,128)S(1)} %get-tuple-element.10, bf16[9600,2]{0,1:T(2,128)(2,1)S(1)} %reshape.12, bf16[1200,9600]{1,0:T(8,128)(2,1)} %param.7), kind=kOutput, calls=%fused_computation.52 | convolution fusion | flops 46084800 | bytes 23097608 | tf_op jit(solution)/shard_map/wq,aq->wa/dot_general | solution.py:52
  170.0 0.2 collective-permute-start.6
  170.2 6.3 %fusion.28 = f32[1200,2,1200]{2,0,1:T(8,128)} fusion(bf16[1200,400]{0,1:T(8,128)(2,1)S(1)} %copy-done.4, bf16[2,400,1200]{2,1,0:T(8,128)(2,1)S(1)} %get-tuple-element.11), kind=kOutput, calls=%fused_computation.44 | convolution fusion | flops 2304000000 | bytes 14400000 | tf_op jit(solution)/shard_map/awi,bi->wab/dot_general | solution.py:42
  176.5 13.4 %copy.22 = f32[1200,2,1200]{0,2,1:T(8,128)} copy(f32[1200,2,1200]{2,0,1:T(8,128)} %fusion.28) | data formatting | bytes 23040000 | tf_op jit(solution)/shard_map/awi,bi->wab/dot_general | solution.py:42
  189.9 10.9 %fusion.8 = f32[2]{0:T(128)S(1)} fusion(f32[1200,2,1200]{2,0,1:T(8,128)} %fusion.28, f32[1200,2,1200]{0,2,1:T(8,128)} %copy.22, f32[1200,1200]{0,1:T(8,128)} %copy.21), kind=kLoop, calls=%fused_computation.17 | loop fusion | flops 8639998 | bytes 28800008 | tf_op jit(solution)/shard_map/reduce_sum | solution.py:49
  200.8 1.5 collective-permute-start.8
  202.3 8.0 %convolution_bitcast_fusion.3 = f32[2,1200,1200]{2,1,0:T(8,128)} fusion(bf16[1200,2,400]{0,2,1:T(8,128)(2,1)} %collective-permute-done.4, bf16[1200,400]{0,1:T(8,128)(2,1)S(1)} %copy-done.4), kind=kOutput, calls=%fused_computation.15 | convolution fusion | flops 2304000000 | bytes 14400000 | tf_op jit(solution)/shard_map/ai,bwi->wab/dot_general | solution.py:43
  210.4 8.6 %fusion.12 = f32[2]{0:T(128)S(1)} fusion(f32[2,1200,1200]{2,1,0:T(8,128)} %convolution_bitcast_fusion.3, f32[1200,1200]{1,0:T(8,128)S(1)} %bitcast.115, bf16[1200,400]{0,1:T(8,128)(2,1)S(1)} %copy-done.6, bf16[2,400,1200]{2,1,0:T(8,128)(2,1)S(1)} %get-tuple-element.11), kind=kOutput, calls=%fused_computation.28 | convolution fusion | flops 2312640000 | bytes 20160008 | tf_op jit(solution)/shard_map/awi,bi->wab/dot_general | solution.py:42
  218.9 8.2 %convolution_bitcast_fusion.2 = f32[2,1200,1200]{2,1,0:T(8,128)} fusion(bf16[1200,2,400]{0,2,1:T(8,128)(2,1)} %collective-permute-done.6, bf16[1200,400]{0,1:T(8,128)(2,1)S(1)} %copy-done.4), kind=kOutput, calls=%fused_computation.14 | convolution fusion | flops 2304000000 | bytes 14400000 | tf_op jit(solution)/shard_map/ai,bwi->wab/dot_general | solution.py:43
  227.1 0.3 collective-permute-start.10
  227.5 8.6 %fusion.11 = f32[2]{0:T(128)S(1)} fusion(f32[2,1200,1200]{2,1,0:T(8,128)} %convolution_bitcast_fusion.2, f32[1200,1200]{1,0:T(8,128)S(1)} %bitcast.113, bf16[1200,400]{0,1:T(8,128)(2,1)S(1)} %copy-done.8, bf16[2,400,1200]{2,1,0:T(8,128)(2,1)S(1)} %copy-done.1), kind=kOutput, calls=%fused_computation.27 | convolution fusion | flops 2312640000 | bytes 20160008 | tf_op jit(solution)/shard_map/awi,bi->wab/dot_general | solution.py:42
  236.1 8.2 %convolution_bitcast_fusion.1 = f32[2,1200,1200]{2,1,0:T(8,128)} fusion(bf16[1200,2,400]{0,2,1:T(8,128)(2,1)} %collective-permute-done.8, bf16[1200,400]{0,1:T(8,128)(2,1)S(1)} %copy-done.4), kind=kOutput, calls=%fused_computation.13 | convolution fusion | flops 2304000000 | bytes 14400000 | tf_op jit(solution)/shard_map/ai,bwi->wab/dot_general | solution.py:43
  244.3 8.9 %fusion.10 = f32[2]{0:T(128)S(1)} fusion(f32[2,1200,1200]{2,1,0:T(8,128)} %convolution_bitcast_fusion.1, f32[1200,1200]{1,0:T(8,128)S(1)} %bitcast.111, bf16[1200,400]{0,1:T(8,128)(2,1)} %collective-permute-done.7, bf16[2,400,1200]{2,1,0:T(8,128)(2,1)S(1)} %copy-done.2), kind=kOutput, calls=%fused_computation.26 | convolution fusion | flops 2312640000 | bytes 20160008 | tf_op jit(solution)/shard_map/awi,bi->wab/dot_general | solution.py:42
  253.3 8.1 %convolution_bitcast_fusion = f32[2,1200,1200]{2,1,0:T(8,128)} fusion(bf16[1200,2,400]{0,2,1:T(8,128)(2,1)} %collective-permute-done.10, bf16[1200,400]{0,1:T(8,128)(2,1)S(1)} %copy-done.4), kind=kOutput, calls=%fused_computation.12 | convolution fusion | flops 2304000000 | bytes 14400000 | tf_op jit(solution)/shard_map/ai,bwi->wab/dot_general | solution.py:43
  261.5 8.7 %fusion.9 = f32[2]{0:T(128)S(1)} fusion(f32[2,1200,1200]{2,1,0:T(8,128)} %convolution_bitcast_fusion, f32[1200,1200]{1,0:T(8,128)S(1)} %bitcast.109, bf16[1200,400]{0,1:T(8,128)(2,1)} %collective-permute-done.9, bf16[2,400,1200]{2,1,0:T(8,128)(2,1)S(1)} %copy-done.2), kind=kOutput, calls=%fused_computation.25 | convolution fusion | flops 2312640000 | bytes 20160008 | tf_op jit(solution)/shard_map/awi,bi->wab/dot_general | solution.py:42
  270.2 14.6 %all-reduce = (f32[2]{0:T(128)}, f32[2]{0:T(128)}) all-reduce(f32[2]{0:T(128)S(1)} %broadcast_multiply_fusion, f32[2]{0:T(128)S(1)} %add_multiply_fusion), channel_id=1, replica_groups=mesh['pts'=8,'wlk'=4] {'pts'}, use_global_device_ids=true, to_apply=%region_1.2 | all-reduce | flops 4 | bytes 32 | tf_op jit(solution)/shard_map/psum | solution.py:63
  (60 shorter events, 0.5 us)
Async XLA Ops:
  0.6 38.3 %collective-permute-start = (bf16[600,1200]{1,0:T(8,128)(2,1)}, bf16[600,1200]{1,0:T(8,128)(2,1)S(1)}, u32[]{:S(2)}, u32[]{:S(2)}) collective-permute-start(bf16[600,1200]{1,0:T(8,128)(2,1)} %param.5), channel_id=1, source_target_pairs={{0,3},{1,0},{2,1},{3,2},{4,7},{5,4},{6,5},{7,6},{8,11},{9,8},{10,9... | collective-permute-start | bytes 4320008 | tf_op jit(solution)/shard_map/ppermute | solution.py:14
  38.9 40.6 %copy-start.10 = (bf16[600,1200]{1,0:T(8,128)(2,1)}, bf16[600,1200]{1,0:T(8,128)(2,1)S(1)}, u32[]{:S(2)}) copy-start(bf16[600,1200]{1,0:T(8,128)(2,1)S(1)} %collective-permute-done) | copy-start | bytes 4320004
  38.9 36.2 %collective-permute-start.1 = (bf16[600,1200]{1,0:T(8,128)(2,1)S(1)}, bf16[600,1200]{1,0:T(8,128)(2,1)}, u32[]{:S(2)}, u32[]{:S(2)}) collective-permute-start(bf16[600,1200]{1,0:T(8,128)(2,1)S(1)} %collective-permute-done), channel_id=1, source_target_pairs={{0,3},{1,0},{2,1},{3,2},{4,7},{5,4},{6,5},{7,6},{8,11},{9,8},{10,9... | collective-permute-start | bytes 4320008 | tf_op jit(solution)/shard_map/ppermute | solution.py:14
  43.1 36.4 %collective-permute-start.3 = (bf16[1200,400]{0,1:T(8,128)(2,1)}, bf16[1200,400]{0,1:T(8,128)(2,1)S(1)}, u32[]{:S(2)}, u32[]{:S(2)}) collective-permute-start(bf16[1200,400]{0,1:T(8,128)(2,1)} %param.6), channel_id=1, source_target_pairs={{28,0},{0,4},{4,8},{8,12},{12,16},{16,20},{20,24},{24,28},{29,1},{... | collective-permute-start | bytes 2880008 | tf_op jit(solution)/shard_map/ppermute | solution.py:22
  75.1 35.9 %collective-permute-start.2 = (bf16[600,1200]{1,0:T(8,128)(2,1)}, bf16[600,1200]{1,0:T(8,128)(2,1)}, u32[]{:S(2)}, u32[]{:S(2)}) collective-permute-start(bf16[600,1200]{1,0:T(8,128)(2,1)} %collective-permute-done.1), channel_id=1, source_target_pairs={{0,3},{1,0},{2,1},{3,2},{4,7},{5,4},{6,5},{7,6},{8,11},{9,8},{10,9... | collective-permute-start | bytes 4320008 | tf_op jit(solution)/shard_map/ppermute | solution.py:14
  79.5 6.8 %copy-start.5 = (bf16[1200,400]{0,1:T(8,128)(2,1)}, bf16[1200,400]{0,1:T(8,128)(2,1)S(1)}, u32[]{:S(2)}) copy-start(bf16[1200,400]{0,1:T(8,128)(2,1)S(1)} %collective-permute-done.3) | copy-start | bytes 2880004
  79.5 14.9 %collective-permute-start.5 = (bf16[1200,400]{0,1:T(8,128)(2,1)S(1)}, bf16[1200,400]{0,1:T(8,128)(2,1)S(1)}, u32[]{:S(2)}, u32[]{:S(2)}) collective-permute-start(bf16[1200,400]{0,1:T(8,128)(2,1)S(1)} %collective-permute-done.3), channel_id=1, source_target_pairs={{28,0},{0,4},{4,8},{8,12},{12,16},{16,20},{20,24},{24,28},{29,1},{... | collective-permute-start | bytes 2880008 | tf_op jit(solution)/shard_map/ppermute | solution.py:22
  82.6 3.8 %copy-start.9 = (bf16[2,400,2400]{2,1,0:T(8,128)(2,1)S(1)}, bf16[2,400,2400]{2,1,0:T(8,128)(2,1)}, u32[]{:S(2)}) copy-start(bf16[2,400,2400]{2,1,0:T(8,128)(2,1)} %param.4) | copy-start | bytes 11520004
  82.6 3.8 %copy-start.11 = (bf16[600,1200]{1,0:T(8,128)(2,1)S(1)}, bf16[600,1200]{1,0:T(8,128)(2,1)}, u32[]{:S(2)}) copy-start(bf16[600,1200]{1,0:T(8,128)(2,1)} %copy-done.10) | copy-start | bytes 4320004
  88.2 22.8 %copy-start.3 = (f32[1200,400]{0,1:T(8,128)S(1)}, f32[1200,400]{0,1:T(8,128)}, u32[]{:S(2)}) copy-start(f32[1200,400]{0,1:T(8,128)} %convert.2) | copy-start | bytes 5760004
  94.4 20.2 %copy-start.7 = (bf16[1200,400]{0,1:T(8,128)(2,1)}, bf16[1200,400]{0,1:T(8,128)(2,1)S(1)}, u32[]{:S(2)}) copy-start(bf16[1200,400]{0,1:T(8,128)(2,1)S(1)} %collective-permute-done.5) | copy-start | bytes 2880004
  94.4 46.2 %collective-permute-start.7 = (bf16[1200,400]{0,1:T(8,128)(2,1)S(1)}, bf16[1200,400]{0,1:T(8,128)(2,1)}, u32[]{:S(2)}, u32[]{:S(2)}) collective-permute-start(bf16[1200,400]{0,1:T(8,128)(2,1)S(1)} %collective-permute-done.5), channel_id=1, source_target_pairs={{28,0},{0,4},{4,8},{8,12},{12,16},{16,20},{20,24},{24,28},{29,1},{... | collective-permute-start | bytes 2880008 | tf_op jit(solution)/shard_map/ppermute | solution.py:22
  114.6 95.7 %copy-start = (bf16[2,400,1200]{2,1,0:T(8,128)(2,1)}, bf16[2,400,1200]{2,1,0:T(8,128)(2,1)S(1)}, u32[]{:S(2)}) copy-start(bf16[2,400,1200]{2,1,0:T(8,128)(2,1)S(1)} %get-tuple-element.11) | copy-start | bytes 5760004
  114.6 55.3 %collective-permute-start.4 = (bf16[1200,2,400]{0,2,1:T(8,128)(2,1)S(1)}, bf16[1200,2,400]{0,2,1:T(8,128)(2,1)}, u32[]{:S(2)}, u32[]{:S(2)}) collective-permute-start(bf16[1200,2,400]{0,2,1:T(8,128)(2,1)S(1)} %bitcast.116), channel_id=1, source_target_pairs={{28,0},{0,4},{4,8},{8,12},{12,16},{16,20},{20,24},{24,28},{29,1},{... | collective-permute-start | bytes 5760008 | tf_op jit(solution)/shard_map/ppermute | solution.py:22
  140.7 120.8 %collective-permute-start.9 = (bf16[1200,400]{0,1:T(8,128)(2,1)}, bf16[1200,400]{0,1:T(8,128)(2,1)}, u32[]{:S(2)}, u32[]{:S(2)}) collective-permute-start(bf16[1200,400]{0,1:T(8,128)(2,1)} %collective-permute-done.7), channel_id=1, source_target_pairs={{28,0},{0,4},{4,8},{8,12},{12,16},{16,20},{20,24},{24,28},{29,1},{... | collective-permute-start | bytes 2880008 | tf_op jit(solution)/shard_map/ppermute | solution.py:22
  158.4 11.7 %copy-start.4 = (bf16[1200,400]{0,1:T(8,128)(2,1)S(1)}, bf16[1200,400]{0,1:T(8,128)(2,1)}, u32[]{:S(2)}) copy-start(bf16[1200,400]{0,1:T(8,128)(2,1)} %param.6) | copy-start | bytes 2880004
  170.0 30.9 %collective-permute-start.6 = (bf16[1200,2,400]{0,2,1:T(8,128)(2,1)}, bf16[1200,2,400]{0,2,1:T(8,128)(2,1)}, u32[]{:S(2)}, u32[]{:S(2)}) collective-permute-start(bf16[1200,2,400]{0,2,1:T(8,128)(2,1)} %collective-permute-done.4), channel_id=1, source_target_pairs={{28,0},{0,4},{4,8},{8,12},{12,16},{16,20},{20,24},{24,28},{29,1},{... | collective-permute-start | bytes 5760008 | tf_op jit(solution)/shard_map/ppermute | solution.py:22
  189.9 20.4 %slice-start.6 = ((s8[6144000]{0:T(1024)(128)(4,1)}), s8[4194304]{0:T(1024)(128)(4,1)S(1)}, s32[]{:S(2)}) async-start(s8[6144000]{0:T(1024)(128)(4,1)} %bitcast.114), calls=%async_computation.6 | async-start | bytes 8388608
  200.8 9.5 %slice-start.7 = ((s8[6144000]{0:T(1024)(128)(4,1)}), s8[1949696]{0:T(1024)(128)(4,1)S(1)}, s32[]{:S(2)}) async-start(s8[6144000]{0:T(1024)(128)(4,1)} %bitcast.114), calls=%async_computation.7 | async-start | bytes 3899392
  200.8 9.5 %copy-start.6 = (bf16[1200,400]{0,1:T(8,128)(2,1)S(1)}, bf16[1200,400]{0,1:T(8,128)(2,1)}, u32[]{:S(2)}) copy-start(bf16[1200,400]{0,1:T(8,128)(2,1)} %copy-done.5) | copy-start | bytes 2880004
  200.8 26.3 %collective-permute-start.8 = (bf16[1200,2,400]{0,2,1:T(8,128)(2,1)}, bf16[1200,2,400]{0,2,1:T(8,128)(2,1)}, u32[]{:S(2)}, u32[]{:S(2)}) collective-permute-start(bf16[1200,2,400]{0,2,1:T(8,128)(2,1)} %collective-permute-done.6), channel_id=1, source_target_pairs={{28,0},{0,4},{4,8},{8,12},{12,16},{16,20},{20,24},{24,28},{29,1},{... | collective-permute-start | bytes 5760008 | tf_op jit(solution)/shard_map/ppermute | solution.py:22
  210.3 17.1 %slice-start.4 = ((s8[6144000]{0:T(1024)(128)(4,1)}), s8[4194304]{0:T(1024)(128)(4,1)S(1)}, s32[]{:S(2)}) async-start(s8[6144000]{0:T(1024)(128)(4,1)} %bitcast.112), calls=%async_computation.4 | async-start | bytes 8388608
  218.9 8.5 %slice-start.5 = ((s8[6144000]{0:T(1024)(128)(4,1)}), s8[1949696]{0:T(1024)(128)(4,1)S(1)}, s32[]{:S(2)}) async-start(s8[6144000]{0:T(1024)(128)(4,1)} %bitcast.112), calls=%async_computation.5 | async-start | bytes 3899392
  218.9 8.5 %copy-start.1 = (bf16[2,400,1200]{2,1,0:T(8,128)(2,1)S(1)}, bf16[2,400,1200]{2,1,0:T(8,128)(2,1)}, u32[]{:S(2)}) copy-start(bf16[2,400,1200]{2,1,0:T(8,128)(2,1)} %copy-done) | copy-start | bytes 5760004
  218.9 8.5 %copy-start.8 = (bf16[1200,400]{0,1:T(8,128)(2,1)S(1)}, bf16[1200,400]{0,1:T(8,128)(2,1)}, u32[]{:S(2)}) copy-start(bf16[1200,400]{0,1:T(8,128)(2,1)} %copy-done.7) | copy-start | bytes 2880004
  227.1 26.1 %collective-permute-start.10 = (bf16[1200,2,400]{0,2,1:T(8,128)(2,1)}, bf16[1200,2,400]{0,2,1:T(8,128)(2,1)}, u32[]{:S(2)}, u32[]{:S(2)}) collective-permute-start(bf16[1200,2,400]{0,2,1:T(8,128)(2,1)} %collective-permute-done.8), channel_id=1, source_target_pairs={{28,0},{0,4},{4,8},{8,12},{12,16},{16,20},{20,24},{24,28},{29,1},{... | collective-permute-start | bytes 5760008 | tf_op jit(solution)/shard_map/ppermute | solution.py:22
  227.5 16.8 %slice-start.2 = ((s8[6144000]{0:T(1024)(128)(4,1)}), s8[4194304]{0:T(1024)(128)(4,1)S(1)}, s32[]{:S(2)}) async-start(s8[6144000]{0:T(1024)(128)(4,1)} %bitcast.110), calls=%async_computation.2 | async-start | bytes 8388608
  236.1 8.2 %slice-start.3 = ((s8[6144000]{0:T(1024)(128)(4,1)}), s8[1949696]{0:T(1024)(128)(4,1)S(1)}, s32[]{:S(2)}) async-start(s8[6144000]{0:T(1024)(128)(4,1)} %bitcast.110), calls=%async_computation.3 | async-start | bytes 3899392
  236.1 8.2 %copy-start.2 = (bf16[2,400,1200]{2,1,0:T(8,128)(2,1)S(1)}, bf16[2,400,1200]{2,1,0:T(8,128)(2,1)}, u32[]{:S(2)}) copy-start(bf16[2,400,1200]{2,1,0:T(8,128)(2,1)} %copy-done) | copy-start | bytes 5760004
  244.3 17.1 %slice-start = ((s8[6144000]{0:T(1024)(128)(4,1)}), s8[4194304]{0:T(1024)(128)(4,1)S(1)}, s32[]{:S(2)}) async-start(s8[6144000]{0:T(1024)(128)(4,1)} %bitcast.108), calls=%async_computation | async-start | bytes 8388608
  253.2 8.2 %slice-start.1 = ((s8[6144000]{0:T(1024)(128)(4,1)}), s8[1949696]{0:T(1024)(128)(4,1)S(1)}, s32[]{:S(2)}) async-start(s8[6144000]{0:T(1024)(128)(4,1)} %bitcast.108), calls=%async_computation.1 | async-start | bytes 3899392
